TPU v7x, 32 devices: a whole 2x2x4 slice. The times are simulated.
32 devices in a mesh: row: 4 (over y, core), col: 8 (over z, x).
Axes of the slice: x: 2, y: 2, z: 4, core: 2. Of those that a mesh axis runs over, the one named last changes fastest.
Arguments:
- demand: bfloat16 [12288, 128], P(('row', 'col')), may hold values from -6 to 6
- tile_data: bfloat16 [4, 8, 128, 128, 128], P('row', 'col'), may hold values from -0.078125 to 0.078125
- tile_row: int32 [4, 8, 128], P('row', 'col'), may hold values from 0 to 12, as said below
- tile_col: int32 [4, 8, 128], P('row', 'col'), may hold values from 0 to 23, as said below
Outputs:
- leontief: bfloat16 [12288, 128], P(('row', 'col'))
Inputs may be any that keep to these rules, and one draw needn't show every extreme that they name: `tile_row`: the value 4 * 3 marks an empty slot. In every index pair the live slots come first and number at least 42; in every draw some index pair has all 128 slots live. Two slots may name the same tile position; their tiles then add. `tile_col`: empty slots carry a column too, which is ignored.
All inputs are finite; a program needn't handle non-finite values.
Results may differ from a plain program's by a relative error of at most 0.018.
Values may be sent and summed in bfloat16 or wider, within the bound.
A program may use at most 64 MiB of HBM per device.

v0:
```python
import functools

import jax
import jax.numpy as jnp
from jax import lax
from jax.experimental import pallas as pl
from jax.experimental.pallas import tpu as pltpu
from jax.sharding import PartitionSpec as P

GROUP = 2
UNROLL = 10
CUTS = 1
MESH = pl.DeviceIdType.MESH


def schedule(rows_ref, cols_ref, plan_vector, local_rows, zero_block, units):
    slots = rows_ref.shape[1]
    width = plan_vector.shape[1]
    square = (slots, slots)
    row_lane = jnp.broadcast_to(rows_ref[...], square)
    row_sub = jnp.transpose(row_lane)
    col_sub = jnp.transpose(jnp.broadcast_to(cols_ref[...], square))[:, 0:1]
    lane = lax.broadcasted_iota(jnp.int32, square, 1)
    sub = lax.broadcasted_iota(jnp.int32, square, 0)
    same = row_lane == row_sub
    prior_sub = jnp.sum(jnp.where(same & (lane < sub), 1, 0), axis=1, keepdims=True)
    prior_lane = jnp.sum(jnp.where(same & (sub < lane), 1, 0), axis=0, keepdims=True)
    opens = jnp.where((prior_lane & (GROUP - 1)) == 0, 1, 0)
    base = jnp.sum(jnp.where(row_lane < row_sub, jnp.broadcast_to(opens, square), 0), axis=1, keepdims=True)
    mine = row_sub[:, 0:1]
    place = jnp.where(mine < local_rows, base * GROUP + prior_sub, -1)
    wide = (slots, width)
    spot = lax.broadcasted_iota(jnp.int32, wide, 1)
    hit = jnp.broadcast_to(place, wide) == spot
    slot = lax.broadcasted_iota(jnp.int32, wide, 0)

    def total(value):
        return jnp.sum(jnp.where(hit, value, 0), axis=0, keepdims=True)

    plan_vector[0:1, :] = total(slot)
    plan_vector[1:2, :] = zero_block + total(jnp.broadcast_to(col_sub - zero_block, wide))
    plan_vector[2:3, :] = 1 - total(jnp.broadcast_to(jnp.where(prior_sub == 0, 1, 0), wide))
    here = jnp.broadcast_to(mine, wide) == spot
    unit = jnp.broadcast_to(lax.shift_right_arithmetic(place, GROUP // 2), wide)
    last = jnp.max(jnp.where(here, unit, -1), axis=0, keepdims=True)
    plan_vector[3:4, :] = jnp.where(last < 0, units, last)


def kernel(n_row, n_col, n_x, units, rows_ref, cols_ref, demand, tile_hbm, out, tiles, panel_a, panel_b, products,
           packed, landed, first, plan_vector, plan, tile_sem, plan_sem, sx, rx, su, ru, sd, rd, sr, rr):
    n_z = n_col // n_x
    span, edge, columns = demand.shape
    zero_block = n_col * span
    depth = edge // CUTS
    pieces = span * CUTS
    row = lax.axis_index("row")
    col = lax.axis_index("col")
    z = col // n_x
    x = col % n_x
    peer = z * n_x + (n_x - 1 - x)
    up_ok = z < n_z - 1
    down_ok = z > 0

    tile_copy = pltpu.make_async_copy(tile_hbm.at[0, 0], tiles, tile_sem)
    tile_copy.start()

    barrier = pltpu.get_barrier_semaphore()

    def greet(r, c):
        pl.semaphore_signal(barrier, inc=1, device_id=(r, c), device_id_type=MESH)

    for step in range(1, n_row):
        greet((row + step) % n_row, col)
    if n_x > 1:
        greet(row, peer)
    pl.when(up_ok)(lambda: greet(row, col + n_x))
    pl.when(down_ok)(lambda: greet(row, col - n_x))

    for panel in (panel_a, panel_b):
        panel[zero_block] = jnp.zeros((edge, columns), panel.dtype)
    products[units] = jnp.zeros((edge, columns), jnp.float32)
    panel_a[pl.ds(col * span, span)] = demand[...]
    greeted = n_row - 1 + (1 if n_x > 1 else 0) + up_ok.astype(jnp.int32) + down_ok.astype(jnp.int32)
    pl.semaphore_wait(barrier, greeted)

    def remote(src, dst, send, recv, target):
        return pltpu.make_async_remote_copy(
            src_ref=src, dst_ref=dst, send_sem=send, recv_sem=recv, device_id=(row, target), device_id_type=MESH
        )

    def gather(turn, own, panel, ready):
        def piece(ref, tile, p):
            return ref.at[tile + p // CUTS, pl.ds((p % CUTS) * depth, depth)]

        def cross(c, offset, p, src=None):
            at = (turn, offset + n_z - 1, p)
            there = piece(panel, c * span, p)
            return remote(there if src is None else piece(src, 0, p), there, sx.at[at], rx.at[at], peer)

        def upward(c, away, p, src=None):
            there = piece(panel, c * span, p)
            here = there if src is None else piece(src, 0, p)
            return remote(here, there, su.at[turn, away, p], ru.at[turn, away + 1, p], col + n_x)

        def downward(c, away, p, src=None):
            there = piece(panel, c * span, p)
            here = there if src is None else piece(src, 0, p)
            return remote(here, there, sd.at[turn, away, p], rd.at[turn, away + 1, p], col - n_x)

        def arrived(c, sem, away, p):
            there = piece(panel, c * span, p)
            remote(there, there, sem.at[turn, away, p], sem.at[turn, away, p], peer).wait_recv()

        for p in range(pieces):
            if p % CUTS == 0:
                ready(p // CUTS)
            pl.when(up_ok)(lambda: upward(col, 0, p, own).start())
            pl.when(down_ok)(lambda: downward(col, 0, p, own).start())
            if n_x > 1:
                cross(col, 0, p, own).start()
        ready(span)
        for away in range(1, n_z):
            for p in range(pieces):

                @pl.when(z >= away)
                def _():
                    c = col - away * n_x
                    arrived(c, ru, away, p)
                    if away + 1 < n_z:
                        pl.when(up_ok)(lambda: upward(c, away, p).start())
                    if n_x > 1:
                        cross(c, -away, p).start()

                @pl.when(z + away < n_z)
                def _():
                    c = col + away * n_x
                    arrived(c, rd, away, p)
                    if away + 1 < n_z:
                        pl.when(down_ok)(lambda: downward(c, away, p).start())
                    if n_x > 1:
                        cross(c, away, p).start()

        if n_x > 1:
            for p in range(pieces):
                cross(peer, 0, p).wait_recv()
                for away in range(1, n_z):
                    pl.when(z >= away)(lambda: cross(peer - away * n_x, -away, p).wait_recv())
                    pl.when(z + away < n_z)(lambda: cross(peer + away * n_x, away, p).wait_recv())

        def drain():
            for p in range(pieces):
                pl.when(up_ok)(lambda: upward(col, 0, p, own).wait_send())
                pl.when(down_ok)(lambda: downward(col, 0, p, own).wait_send())
                if n_x > 1:
                    cross(col, 0, p, own).wait_send()
                for away in range(1, n_z):

                    @pl.when(z >= away)
                    def _():
                        c = col - away * n_x
                        if n_x > 1:
                            cross(c, -away, p).wait_send()
                        if away + 1 < n_z:
                            pl.when(up_ok)(lambda: upward(c, away, p).wait_send())

                    @pl.when(z + away < n_z)
                    def _():
                        c = col + away * n_x
                        if n_x > 1:
                            cross(c, away, p).wait_send()
                        if away + 1 < n_z:
                            pl.when(down_ok)(lambda: downward(c, away, p).wait_send())

        return drain

    def compute(panel):
        def body(step, total):
            for part in range(UNROLL):
                unit = step * UNROLL + part
                left = [tiles[plan[0, unit * GROUP + k]] for k in range(GROUP)]
                right = [panel[plan[1, unit * GROUP + k]] for k in range(GROUP)]
                keep = plan[2, unit * GROUP].astype(jnp.float32)
                total = total * keep + jnp.dot(
                    jnp.concatenate(left, axis=1), jnp.concatenate(right, axis=0), preferred_element_type=jnp.float32
                )
                products[unit] = total
            return total

        lax.fori_loop(0, units // UNROLL, body, jnp.zeros((edge, columns), jnp.float32))

    def send(turn, step, k):
        r = (row + step) % n_row
        return pltpu.make_async_remote_copy(
            src_ref=packed.at[turn, r * span + k],
            dst_ref=landed.at[turn, step - 1, k],
            send_sem=sr.at[turn, step - 1, k],
            recv_sem=rr.at[turn, step - 1, k],
            device_id=(r, col),
            device_id_type=MESH,
        )

    def scatter(turn):
        steps = sorted(range(1, n_row), key=lambda step: abs(step - n_row // 2))
        for k in range(span):
            for step in steps:
                r = (row + step) % n_row
                packed[turn, r * span + k] = products[plan[3, r * span + k]].astype(packed.dtype)
                send(turn, step, k).start()

        def drain():
            for k in range(span):
                for step in steps:
                    send(turn, step, k).wait_send()

        return drain

    def collect(turn, k):
        value = products[plan[3, row * span + k]]
        for step in range(1, n_row):
            send(turn, step, k).wait_recv()
            value = value + landed[turn, step - 1, k].astype(jnp.float32)
        return value.astype(first.dtype)

    def ready_a(k):
        if k == span:
            schedule(rows_ref, cols_ref, plan_vector, n_row * span, zero_block, units)
            plan_copy = pltpu.make_async_copy(plan_vector, plan, plan_sem)
            plan_copy.start()
            plan_copy.wait()

    def ready_b(k):
        if k < span:
            value = collect(0, k)
            first[k] = value
            panel_b[col * span + k] = value

    drains = [gather(0, demand, panel_a, ready_a)]
    tile_copy.wait()
    compute(panel_a)
    drains.append(scatter(0))
    drains.append(gather(1, first, panel_b, ready_b))
    compute(panel_b)
    drains.append(scatter(1))
    for k in range(span):
        value = collect(1, k)
        out[k] = (
            demand[k].astype(jnp.float32) + first[k].astype(jnp.float32) + value.astype(jnp.float32)
        ).astype(out.dtype)
    for drain in drains:
        drain()


def body(n_row, n_col, demand, tile_data, tile_row, tile_col):
    slots, edge = tile_data.shape[2], tile_data.shape[-1]
    columns = demand.shape[1]
    span = demand.shape[0] // edge
    local_rows = n_row * span
    n_x = 2 if n_col % 2 == 0 else 1
    n_z = n_col // n_x
    units = (slots + local_rows * (GROUP - 1)) // GROUP
    units = -(-units // UNROLL) * UNROLL
    width = -(-max(units * GROUP, local_rows) // 128) * 128
    pieces = span * CUTS
    dma = pltpu.SemaphoreType.DMA
    vmem = pl.BlockSpec(memory_space=pltpu.VMEM)
    result = pl.pallas_call(
        functools.partial(kernel, n_row, n_col, n_x, units),
        out_shape=jax.ShapeDtypeStruct((span, edge, columns), demand.dtype),
        in_specs=[vmem, vmem, vmem, pl.BlockSpec(memory_space=pl.ANY)],
        out_specs=vmem,
        scratch_shapes=[
            pltpu.VMEM((slots, edge, edge), tile_data.dtype),
            pltpu.VMEM((n_col * span + 1, edge, columns), demand.dtype),
            pltpu.VMEM((n_col * span + 1, edge, columns), demand.dtype),
            pltpu.VMEM((units + 1, edge, columns), jnp.float32),
            pltpu.VMEM((2, local_rows, edge, columns), demand.dtype),
            pltpu.VMEM((2, n_row - 1, span, edge, columns), demand.dtype),
            pltpu.VMEM((span, edge, columns), demand.dtype),
            pltpu.VMEM((8, width), jnp.int32),
            pltpu.SMEM((8, width), jnp.int32),
            dma,
            dma,
            dma((2, 2 * n_z - 1, pieces)),
            dma((2, 2 * n_z - 1, pieces)),
            dma((2, n_z + 1, pieces)),
            dma((2, n_z + 1, pieces)),
            dma((2, n_z + 1, pieces)),
            dma((2, n_z + 1, pieces)),
            dma((2, n_row - 1, span)),
            dma((2, n_row - 1, span)),
        ],
        compiler_params=pltpu.CompilerParams(
            collective_id=0, has_side_effects=True, vmem_limit_bytes=56 * 1024 * 1024
        ),
    )(tile_row[0], tile_col[0], demand.reshape(span, edge, columns), tile_data)
    return result.reshape(demand.shape)


def solution(mesh):
    placed = (
        P(("row", "col"), None),
        P("row", "col", None, None, None),
        P("row", "col", None),
        P("row", "col", None),
    )
    return jax.shard_map(
        functools.partial(body, mesh.shape["row"], mesh.shape["col"]),
        mesh=mesh, in_specs=placed, out_specs=P(("row", "col"), None), check_vma=False,
    )
```

profile of v0, /device:TPU:0, one launch (start us, length us, event | category | flops | bytes accessed | tf_op | source)
XLA Modules:
  0.0 47.4 jit_solution(6259182087056835452)
XLA Ops:
  0.0 45.9 %shard_map.46 = bf16[3,128,128]{2,1,0:T(8,128)(2,1)} custom-call(s32[1,128]{1,0:T(1,128)} %bitcast.6, s32[1,128]{1,0:T(1,128)} %bitcast.7, bf16[3,128,128]{2,1,0:T(8,128)(2,1)} %bitcast.5, bf16[1,1,128,128,128]{4,3,2,1,0:T(8,128)(2,1)} %tile_hbm.1), custom_call_target="tpu_custom_call" | custom-call | tf_op jit(solution)/shard_map/pallas_call | solution.py:266
  45.9 1.5 %copy.6 = bf16[384,128]{1,0:T(8,128)(2,1)} copy(bf16[384,128]{1,0:T(8,128)(2,1)} %bitcast.4) | data formatting | bytes 196608
where the time goes:
time: 47.6 us; the launch traced here: 47.4 us
  Pallas kernels  45.9 us (96%)
  local copies, waits for them, and re-layouts  1.54 us (3%)
    pallas_call x1, Pallas kernels, body(): pl.pallas_call(functools.partial(kernel, n_row, n_col, n_x, units), out_s...  45.9 us
    unnamed x1, local copies, waits for them, and re-layouts  1.54 us

commit v1 on v0

v1 whole, which is shorter than its diff:
```python
import functools

import jax
import jax.numpy as jnp
from jax import lax
from jax.experimental import pallas as pl
from jax.experimental.pallas import tpu as pltpu
from jax.sharding import PartitionSpec as P

CHUNKS = 4
BUILD = 8
MESH = pl.DeviceIdType.MESH


def schedule(rows_ref, cols_ref, plan_vector, local_rows, source_tiles):
    slots = rows_ref.shape[1]
    width = plan_vector.shape[1]
    square, wide = (slots, slots), (slots, width)
    key_lane = jnp.broadcast_to(rows_ref[...] * source_tiles + cols_ref[...], square)
    key_sub = jnp.transpose(key_lane)
    lane = lax.broadcasted_iota(jnp.int32, square, 1)
    sub = lax.broadcasted_iota(jnp.int32, square, 0)
    prior = (key_lane == key_sub) & (lane < sub)
    place = jnp.sum(jnp.where((key_lane < key_sub) | prior, 1, 0), axis=1, keepdims=True)
    repeats = jnp.sum(jnp.where(prior, 1, 0), axis=1, keepdims=True)
    hit = jnp.broadcast_to(place, square) == lane

    def total(value):
        return jnp.sum(jnp.where(hit, value, 0), axis=0, keepdims=True)

    spot = lax.broadcasted_iota(jnp.int32, wide, 1)
    here = jnp.broadcast_to(key_sub[:, 0:1], wide) == spot
    last = jnp.max(jnp.where(here, jnp.broadcast_to(place, wide), -1), axis=0, keepdims=True)
    plan_vector[0:1, :] = jnp.where(last < 0, slots, last)
    plan_vector[1:2, 0:slots] = total(sub)
    plan_vector[2:3, 0:slots] = total(jnp.broadcast_to(jnp.where(repeats == 0, 0, 1), square))


def order_of(chunks):
    ops = [("Z", 0, 0), ("S", 0, 0)]
    for c in range(1, chunks):
        ops += [("Z", 0, c), ("X", 0, c - 1), ("S", 0, c)]
        if c >= 3:
            ops += [("E", 0, c - 3)]
    ops += [("X", 0, chunks - 1)]
    ops += [("E", 0, c) for c in range(max(chunks - 3, 0), chunks - 1)]
    ops += [("Z", 1, 0), ("S", 1, 0), ("E", 0, chunks - 1)]
    for c in range(1, chunks):
        ops += [("Z", 1, c), ("X", 1, c - 1), ("S", 1, c)]
        if c >= 3:
            ops += [("E", 1, c - 3)]
    ops += [("X", 1, chunks - 1)]
    ops += [("E", 1, c) for c in range(max(chunks - 3, 0), chunks)]
    return ops


def kernel(n_row, n_col, n_x, rows_ref, cols_ref, demand, tile_hbm, out, tiles, weights, panel_a, panel_b, sums,
           packed, landed, out_turned, plan_vector, plan, tile_sem, plan_sem, sx, rx, sz, rz, sr, rr):
    n_z = n_col // n_x
    span, edge, columns = demand.shape
    slots = tiles.shape[0]
    source_tiles = n_col * span
    local_rows = n_row * span
    panels = (panel_a, panel_b)
    chunks, part = panel_a.shape[0], panel_a.shape[2]
    row = lax.axis_index("row")
    col = lax.axis_index("col")
    z = col // n_x
    x = col % n_x
    other = n_x - 1 - x
    paired = n_z & (n_z - 1) == 0
    cores = 2 if n_row % 2 == 0 else 1
    n_y = n_row // cores

    tile_copy = pltpu.make_async_copy(tile_hbm.at[0, 0], tiles, tile_sem)
    tile_copy.start()

    def flipped(value, k):
        bit, result = 1, value
        while bit <= k:
            if k & bit:
                result = result + bit - 2 * bit * ((value // bit) % 2)
            bit *= 2
        return result

    def sent_to(k):
        return flipped(z, k) if paired else (z + k) % n_z

    def got_from(k):
        return flipped(z, k) if paired else (z + n_z - k) % n_z

    def target(e):
        return ((row // cores + 1 + e // cores) % n_y) * cores + (row % cores + 1 + e % cores) % cores

    barrier = pltpu.get_barrier_semaphore()

    def greet(r, c):
        pl.semaphore_signal(barrier, inc=1, device_id=(r, c), device_id_type=MESH)

    for k in range(1, n_z):
        greet(row, sent_to(k) * n_x + x)
    for e in range(n_row - 1):
        greet(target(e), col)
    if n_x > 1:
        greet(row, z * n_x + other)

    for k in range(span):
        turned = jnp.transpose(demand[k])
        for c in range(chunks):
            panel_a[c, col * span + k] = turned[c * part:(c + 1) * part]
    pl.semaphore_wait(barrier, n_z - 1 + n_row - 1 + (1 if n_x > 1 else 0))

    def block(p, c, zz, xx):
        return panels[p].at[c, pl.ds((zz * n_x + xx) * span, span)]

    def remote(src, dst, send, recv, device):
        return pltpu.make_async_remote_copy(
            src_ref=src, dst_ref=dst, send_sem=send, recv_sem=recv, device_id=device, device_id_type=MESH
        )

    def across(p, c, k):
        here = block(p, c, got_from(k) if k else z, x)
        return remote(here, here, sx.at[p, c, k], rx.at[p, c, k], (row, z * n_x + other))

    def across_in(p, c, k):
        here = block(p, c, got_from(k) if k else z, other)
        remote(here, here, sx.at[p, c, k], rx.at[p, c, k], (row, z * n_x + other)).wait_recv()

    def along(p, c, k):
        here = block(p, c, z, x)
        return remote(here, here, sz.at[p, c, k - 1], rz.at[p, c, k - 1], (row, sent_to(k) * n_x + x))

    def along_in(p, c, k):
        here = block(p, c, got_from(k), x)
        remote(here, here, sz.at[p, c, k - 1], rz.at[p, c, k - 1], (row, sent_to(k) * n_x + x)).wait_recv()

    def reduce_copy(p, c, e):
        return remote(packed.at[p, c, pl.ds(e * span, span)], landed.at[p, c, e], sr.at[p, c, e], rr.at[p, c, e],
                      (target(e), col))

    def launch(p, c):
        if n_x > 1:
            across(p, c, 0).start()
        for k in reversed(range(1, n_z)):
            along(p, c, k).start()

    def relay(p, c):
        for k in range(1, n_z):
            along_in(p, c, k)
            if n_x > 1:
                across(p, c, k).start()

    def product(p, c, sources, first, final):
        held = [block_tile for source in sources for block_tile in [source * span + k for k in range(span)]]
        deep = [held[i:i + 2] for i in range(0, len(held), 2)]
        left = [jnp.concatenate([panels[p][c, t] for t in group], axis=1) for group in deep]

        def unit(u):
            places = [u * cores * span + q for q in range(cores * span)]
            for at in range(0, len(places), 2):
                pair = places[at:at + 2]
                home = [target(q // span) * span + q % span for q in pair]
                total = None
                for group, value in zip(deep, left):
                    right = jnp.concatenate(
                        [jnp.concatenate([weights[plan[0, h * source_tiles + t]] for t in group], axis=0) for h in home],
                        axis=1,
                    )
                    term = jnp.dot(value, right, preferred_element_type=jnp.float32)
                    total = term if total is None else total + term
                for i, q in enumerate(pair):
                    value = total[:, i * edge:(i + 1) * edge]
                    if not first:
                        value = value + sums[c, q]
                    static = isinstance(q, int)
                    if not final or not static or q >= (n_row - 1) * span:
                        sums[c, q] = value
                    if final and (not static or q < (n_row - 1) * span):
                        packed[p, c, q] = value.astype(packed.dtype)
            if final:
                for i in range(cores):
                    e = u * cores + i
                    if isinstance(e, int):
                        if e < n_row - 1:
                            reduce_copy(p, c, e).start()
                    else:
                        pl.when(e < n_row - 1)(lambda: reduce_copy(p, c, e).start())

        if n_y <= 2:
            for u in range(n_y):
                unit(u)
        else:
            lax.fori_loop(0, n_y, lambda u, _: (unit(u), 0)[1], 0)

    def near(p, c):
        product(p, c, [(got_from(k) if k else z) * n_x + x for k in range(n_z)], True, n_x == 1)

    def far(p, c):
        if n_x > 1:
            half = n_z // 2 if n_z > 1 else n_z
            for lo, hi in ((0, half), (half, n_z)):
                if lo < hi:
                    for k in range(lo, hi):
                        across_in(p, c, k)
                    product(p, c, [(got_from(k) if k else z) * n_x + other for k in range(lo, hi)], False, hi == n_z)

    def collect(p, c):
        for e in range(n_row - 1):
            reduce_copy(p, c, e).wait_recv()
        for k in range(span):
            value = sums[c, (n_row - 1) * span + k]
            for e in range(n_row - 1):
                value = value + landed[p, c, e, k].astype(jnp.float32)
            value = value.astype(panel_b.dtype)
            mine = col * span + k
            if p == 0:
                panel_b[c, mine] = value
            else:
                out_turned[k, c * part:(c + 1) * part] = (
                    panel_a[c, mine].astype(jnp.float32) + panel_b[c, mine].astype(jnp.float32)
                    + value.astype(jnp.float32)
                ).astype(out.dtype)
        if p == 0:
            launch(1, c)

    for c in range(chunks):
        launch(0, c)

    schedule(rows_ref, cols_ref, plan_vector, local_rows, source_tiles)
    plan_copy = pltpu.make_async_copy(plan_vector, plan, plan_sem)
    plan_copy.start()
    weights[slots] = jnp.zeros((edge, edge), weights.dtype)
    plan_copy.wait()
    tile_copy.wait()

    def merge(step, total):
        for u in range(BUILD):
            at = step * BUILD + u
            keep = plan[2, at].astype(jnp.float32)
            total = total * keep + tiles[plan[1, at]].astype(jnp.float32)
            weights[at] = jnp.transpose(total.astype(weights.dtype))
        return total

    lax.fori_loop(0, slots // BUILD, merge, jnp.zeros((edge, edge), jnp.float32))

    act = {"Z": relay, "S": near, "X": far, "E": collect}
    for op, p, c in order_of(chunks):
        act[op](p, c)

    for k in range(span):
        out[k] = jnp.transpose(out_turned[k])
    for p in range(2):
        for c in range(chunks):
            for k in range(n_z):
                if n_x > 1:
                    across(p, c, k).wait_send()
                if k:
                    along(p, c, k).wait_send()
            for e in range(n_row - 1):
                reduce_copy(p, c, e).wait_send()


def body(n_row, n_col, demand, tile_data, tile_row, tile_col):
    slots, edge = tile_data.shape[2], tile_data.shape[-1]
    columns = demand.shape[1]
    span = demand.shape[0] // edge
    local_rows = n_row * span
    n_x = 2 if n_col % 2 == 0 else 1
    n_z = n_col // n_x
    part = columns // CHUNKS
    width = -(-max(local_rows * n_col * span, slots) // 128) * 128
    dma = pltpu.SemaphoreType.DMA
    kind = demand.dtype
    vmem = pl.BlockSpec(memory_space=pltpu.VMEM)
    result = pl.pallas_call(
        functools.partial(kernel, n_row, n_col, n_x),
        out_shape=jax.ShapeDtypeStruct((span, edge, columns), kind),
        in_specs=[vmem, vmem, vmem, pl.BlockSpec(memory_space=pl.ANY)],
        out_specs=vmem,
        scratch_shapes=[
            pltpu.VMEM((slots, edge, edge), tile_data.dtype),
            pltpu.VMEM((slots + 1, edge, edge), tile_data.dtype),
            pltpu.VMEM((CHUNKS, n_col * span, part, edge), kind),
            pltpu.VMEM((CHUNKS, n_col * span, part, edge), kind),
            pltpu.VMEM((CHUNKS, local_rows, part, edge), jnp.float32),
            pltpu.VMEM((2, CHUNKS, local_rows, part, edge), kind),
            pltpu.VMEM((2, CHUNKS, n_row - 1, span, part, edge), kind),
            pltpu.VMEM((span, columns, edge), kind),
            pltpu.VMEM((8, width), jnp.int32),
            pltpu.SMEM((8, width), jnp.int32),
            dma,
            dma,
            dma((2, CHUNKS, n_z)),
            dma((2, CHUNKS, n_z)),
            dma((2, CHUNKS, n_z)),
            dma((2, CHUNKS, n_z)),
            dma((2, CHUNKS, n_row - 1)),
            dma((2, CHUNKS, n_row - 1)),
        ],
        compiler_params=pltpu.CompilerParams(
            collective_id=0, has_side_effects=True, vmem_limit_bytes=56 * 1024 * 1024
        ),
    )(tile_row[0], tile_col[0], demand.reshape(span, edge, columns), tile_data)
    return result.reshape(demand.shape)


def solution(mesh):
    placed = (
        P(("row", "col"), None),
        P("row", "col", None, None, None),
        P("row", "col", None),
        P("row", "col", None),
    )
    return jax.shard_map(
        functools.partial(body, mesh.shape["row"], mesh.shape["col"]),
        mesh=mesh, in_specs=placed, out_specs=P(("row", "col"), None), check_vma=False,
    )
```

time: 47.6 us -> 43.7 us (0.918)
  Pallas kernels: 45.9 us -> 42 us
    pallas_call x1, Pallas kernels: 45.9 us -> 42 us  [body(): pl.pallas_call(functools.partial(kernel, n_row, n_col, n_x), out_shape=ja...]
where the time goes in v1:
time: 43.7 us; the launch traced here: 43.6 us
  Pallas kernels  42 us (96%)
  local copies, waits for them, and re-layouts  1.54 us (4%)
    pallas_call x1, Pallas kernels, body(): pl.pallas_call(functools.partial(kernel, n_row, n_col, n_x), out_shape=ja...  42 us
    unnamed x1, local copies, waits for them, and re-layouts  1.54 us

profile of v1, /device:TPU:0, one launch (start us, length us, event | category | flops | bytes accessed | tf_op | source)
XLA Modules:
  0.0 43.6 jit_solution(12965209474871764038)
XLA Ops:
  0.0 42.0 %shard_map.46 = bf16[3,128,128]{2,1,0:T(8,128)(2,1)} custom-call(s32[1,128]{1,0:T(1,128)} %bitcast.6, s32[1,128]{1,0:T(1,128)} %bitcast.7, bf16[3,128,128]{2,1,0:T(8,128)(2,1)} %bitcast.5, bf16[1,1,128,128,128]{4,3,2,1,0:T(8,128)(2,1)} %tile_hbm.1), custom_call_target="tpu_custom_call" | custom-call | tf_op jit(solution)/shard_map/pallas_call | solution.py:275
  42.0 1.5 %copy.6 = bf16[384,128]{1,0:T(8,128)(2,1)} copy(bf16[384,128]{1,0:T(8,128)(2,1)} %bitcast.4) | data formatting | bytes 196608

commit v2 on v1

--- a/solution.py
+++ b/solution.py
@@ -9,6 +9,15 @@
 
 CHUNKS = 4
 BUILD = 8
+EARLY = 6
+ORDER = (
+    "Z002", "Z000", "Z001", "S001", "Z010", "Z011", "Z012", "S011", "Z022", "X000", "X001",
+    "Z021", "Z020", "S021", "X010", "Z032", "Z031", "X011", "Z030", "S031", "E000", "X020",
+    "X021", "E010", "X030", "X031", "E020", "Z100", "Z102", "Z101", "S101", "Z110", "Z112",
+    "E030", "Z111", "S111", "Z121", "X100", "X101", "Z120", "Z122", "X110", "Z130", "X111",
+    "Z131", "Z132", "S121", "S131", "X120", "X121", "X130", "X131", "E110", "E100", "E120",
+    "E130",
+)
 MESH = pl.DeviceIdType.MESH
 
 
@@ -36,26 +45,12 @@
     plan_vector[2:3, 0:slots] = total(jnp.broadcast_to(jnp.where(repeats == 0, 0, 1), square))
 
 
-def order_of(chunks):
-    ops = [("Z", 0, 0), ("S", 0, 0)]
-    for c in range(1, chunks):
-        ops += [("Z", 0, c), ("X", 0, c - 1), ("S", 0, c)]
-        if c >= 3:
-            ops += [("E", 0, c - 3)]
-    ops += [("X", 0, chunks - 1)]
-    ops += [("E", 0, c) for c in range(max(chunks - 3, 0), chunks - 1)]
-    ops += [("Z", 1, 0), ("S", 1, 0), ("E", 0, chunks - 1)]
-    for c in range(1, chunks):
-        ops += [("Z", 1, c), ("X", 1, c - 1), ("S", 1, c)]
-        if c >= 3:
-            ops += [("E", 1, c - 3)]
-    ops += [("X", 1, chunks - 1)]
-    ops += [("E", 1, c) for c in range(max(chunks - 3, 0), chunks)]
-    return ops
-
-
-def kernel(n_row, n_col, n_x, rows_ref, cols_ref, demand, tile_hbm, out, tiles, weights, panel_a, panel_b, sums,
-           packed, landed, out_turned, plan_vector, plan, tile_sem, plan_sem, sx, rx, sz, rz, sr, rr):
+def order_of():
+    return [(word[0], int(word[1]), int(word[2]), int(word[3])) for word in ORDER]
+
+
+def kernel(n_row, n_col, n_x, rows_hbm, cols_hbm, demand_hbm, tile_hbm, out, rows_ref, cols_ref, demand, tiles, weights, panel_a, panel_b, sums,
+           packed, landed, out_turned, plan_vector, plan, copy_sem, plan_sem, sx, rx, sz, rz, sr, rr):
     n_z = n_col // n_x
     span, edge, columns = demand.shape
     slots = tiles.shape[0]
@@ -72,8 +67,15 @@
     cores = 2 if n_row % 2 == 0 else 1
     n_y = n_row // cores
 
-    tile_copy = pltpu.make_async_copy(tile_hbm.at[0, 0], tiles, tile_sem)
-    tile_copy.start()
+    copies = [
+        pltpu.make_async_copy(source, there, copy_sem.at[i])
+        for i, (source, there) in enumerate(
+            ((demand_hbm, demand), (rows_hbm, rows_ref), (cols_hbm, cols_ref), (tile_hbm.at[0, 0], tiles))
+        )
+    ]
+    demand_copy, rows_copy, cols_copy, tile_copy = copies
+    for copy in copies:
+        copy.start()
 
     def flipped(value, k):
         bit, result = 1, value
@@ -104,10 +106,31 @@
     if n_x > 1:
         greet(row, z * n_x + other)
 
+    rows_copy.wait()
+    cols_copy.wait()
+    schedule(rows_ref, cols_ref, plan_vector, local_rows, source_tiles)
+    plan_copy = pltpu.make_async_copy(plan_vector, plan, plan_sem)
+    plan_copy.start()
+    weights[slots] = jnp.zeros((edge, edge), weights.dtype)
+    demand_copy.wait()
     for k in range(span):
         turned = jnp.transpose(demand[k])
         for c in range(chunks):
             panel_a[c, col * span + k] = turned[c * part:(c + 1) * part]
+    plan_copy.wait()
+    tile_copy.wait()
+
+    def merge(step, total):
+        for u in range(BUILD):
+            at = step * BUILD + u
+            keep = plan[2, at].astype(jnp.float32)
+            total = total * keep + tiles[plan[1, at]].astype(jnp.float32)
+            weights[at] = jnp.transpose(total.astype(weights.dtype))
+        return total
+
+    steps = slots // BUILD
+    early = steps * EARLY // 8
+    running = lax.fori_loop(0, early, merge, jnp.zeros((edge, edge), jnp.float32))
     pl.semaphore_wait(barrier, n_z - 1 + n_row - 1 + (1 if n_x > 1 else 0))
 
     def block(p, c, zz, xx):
@@ -144,16 +167,19 @@
         for k in reversed(range(1, n_z)):
             along(p, c, k).start()
 
-    def relay(p, c):
-        for k in range(1, n_z):
+    def relay(p, c, at):
+        for k in range(1, n_z)[(n_z - 1) * at // 3:(n_z - 1) * (at + 1) // 3]:
             along_in(p, c, k)
             if n_x > 1:
                 across(p, c, k).start()
 
-    def product(p, c, sources, first, final):
+    def product(p, group, sources, first, final):
         held = [block_tile for source in sources for block_tile in [source * span + k for k in range(span)]]
         deep = [held[i:i + 2] for i in range(0, len(held), 2)]
-        left = [jnp.concatenate([panels[p][c, t] for t in group], axis=1) for group in deep]
+        left = [
+            jnp.concatenate([jnp.concatenate([panels[p][c, t] for t in near], axis=1) for c in group], axis=0)
+            for near in deep
+        ]
 
         def unit(u):
             places = [u * cores * span + q for q in range(cores * span)]
@@ -161,30 +187,31 @@
                 pair = places[at:at + 2]
                 home = [target(q // span) * span + q % span for q in pair]
                 total = None
-                for group, value in zip(deep, left):
+                for near, value in zip(deep, left):
                     right = jnp.concatenate(
-                        [jnp.concatenate([weights[plan[0, h * source_tiles + t]] for t in group], axis=0) for h in home],
+                        [jnp.concatenate([weights[plan[0, h * source_tiles + t]] for t in near], axis=0) for h in home],
                         axis=1,
                     )
                     term = jnp.dot(value, right, preferred_element_type=jnp.float32)
                     total = term if total is None else total + term
                 for i, q in enumerate(pair):
-                    value = total[:, i * edge:(i + 1) * edge]
-                    if not first:
-                        value = value + sums[c, q]
-                    static = isinstance(q, int)
-                    if not final or not static or q >= (n_row - 1) * span:
-                        sums[c, q] = value
-                    if final and (not static or q < (n_row - 1) * span):
-                        packed[p, c, q] = value.astype(packed.dtype)
+                    for j, c in enumerate(group):
+                        value = total[j * part:(j + 1) * part, i * edge:(i + 1) * edge]
+                        if not first:
+                            value = value + sums[c, q]
+                        static = isinstance(q, int)
+                        if not final or not static or q >= (n_row - 1) * span:
+                            sums[c, q] = value
+                        if final and (not static or q < (n_row - 1) * span):
+                            packed[p, c, q] = value.astype(packed.dtype)
             if final:
-                for i in range(cores):
+                for i, c in [(i, c) for i in range(cores) for c in group]:
                     e = u * cores + i
                     if isinstance(e, int):
                         if e < n_row - 1:
                             reduce_copy(p, c, e).start()
                     else:
-                        pl.when(e < n_row - 1)(lambda: reduce_copy(p, c, e).start())
+                        pl.when(e < n_row - 1)(functools.partial(lambda c, e: reduce_copy(p, c, e).start(), c, e))
 
         if n_y <= 2:
             for u in range(n_y):
@@ -192,19 +219,17 @@
         else:
             lax.fori_loop(0, n_y, lambda u, _: (unit(u), 0)[1], 0)
 
-    def near(p, c):
-        product(p, c, [(got_from(k) if k else z) * n_x + x for k in range(n_z)], True, n_x == 1)
-
-    def far(p, c):
-        if n_x > 1:
-            half = n_z // 2 if n_z > 1 else n_z
-            for lo, hi in ((0, half), (half, n_z)):
-                if lo < hi:
-                    for k in range(lo, hi):
-                        across_in(p, c, k)
-                    product(p, c, [(got_from(k) if k else z) * n_x + other for k in range(lo, hi)], False, hi == n_z)
-
-    def collect(p, c):
+    def near(p, c, at):
+        product(p, range(c, c + at), [(got_from(k) if k else z) * n_x + x for k in range(n_z)], True, n_x == 1)
+
+    def far(p, c, at):
+        lo, hi = n_z * at // 2, n_z * (at + 1) // 2
+        if n_x > 1 and lo < hi:
+            for k in range(lo, hi):
+                across_in(p, c, k)
+            product(p, [c], [(got_from(k) if k else z) * n_x + other for k in range(lo, hi)], False, hi == n_z)
+
+    def collect(p, c, at):
         for e in range(n_row - 1):
             reduce_copy(p, c, e).wait_recv()
         for k in range(span):
@@ -226,26 +251,12 @@
     for c in range(chunks):
         launch(0, c)
 
-    schedule(rows_ref, cols_ref, plan_vector, local_rows, source_tiles)
-    plan_copy = pltpu.make_async_copy(plan_vector, plan, plan_sem)
-    plan_copy.start()
-    weights[slots] = jnp.zeros((edge, edge), weights.dtype)
-    plan_copy.wait()
-    tile_copy.wait()
-
-    def merge(step, total):
-        for u in range(BUILD):
-            at = step * BUILD + u
-            keep = plan[2, at].astype(jnp.float32)
-            total = total * keep + tiles[plan[1, at]].astype(jnp.float32)
-            weights[at] = jnp.transpose(total.astype(weights.dtype))
-        return total
-
-    lax.fori_loop(0, slots // BUILD, merge, jnp.zeros((edge, edge), jnp.float32))
+    if early < steps:
+        lax.fori_loop(early, steps, merge, running)
 
     act = {"Z": relay, "S": near, "X": far, "E": collect}
-    for op, p, c in order_of(chunks):
-        act[op](p, c)
+    for op, p, c, at in order_of():
+        act[op](p, c, at)
 
     for k in range(span):
         out[k] = jnp.transpose(out_turned[k])
@@ -275,9 +286,12 @@
     result = pl.pallas_call(
         functools.partial(kernel, n_row, n_col, n_x),
         out_shape=jax.ShapeDtypeStruct((span, edge, columns), kind),
-        in_specs=[vmem, vmem, vmem, pl.BlockSpec(memory_space=pl.ANY)],
+        in_specs=[pl.BlockSpec(memory_space=pl.ANY)] * 4,
         out_specs=vmem,
         scratch_shapes=[
+            pltpu.VMEM((1, slots), jnp.int32),
+            pltpu.VMEM((1, slots), jnp.int32),
+            pltpu.VMEM((span, edge, columns), kind),
             pltpu.VMEM((slots, edge, edge), tile_data.dtype),
             pltpu.VMEM((slots + 1, edge, edge), tile_data.dtype),
             pltpu.VMEM((CHUNKS, n_col * span, part, edge), kind),
@@ -288,7 +302,7 @@
             pltpu.VMEM((span, columns, edge), kind),
             pltpu.VMEM((8, width), jnp.int32),
             pltpu.SMEM((8, width), jnp.int32),
-            dma,
+            dma((4,)),
             dma,
             dma((2, CHUNKS, n_z)),
             dma((2, CHUNKS, n_z)),
@@ -298,9 +312,12 @@
             dma((2, CHUNKS, n_row - 1)),
         ],
         compiler_params=pltpu.CompilerParams(
-            collective_id=0, has_side_effects=True, vmem_limit_bytes=56 * 1024 * 1024
+            collective_id=0, has_side_effects=True, vmem_limit_bytes=28 * 1024 * 1024
         ),
-    )(tile_row[0], tile_col[0], demand.reshape(span, edge, columns), tile_data)
+    )(*(
+        pltpu.with_memory_space_constraint(operand, pltpu.HBM)
+        for operand in (tile_row[0], tile_col[0], demand.reshape(span, edge, columns), tile_data)
+    ))
     return result.reshape(demand.shape)
 
 

time: 43.7 us -> 40.6 us (0.929)
  Pallas kernels: 42 us -> 39.8 us
  local copies, waits for them, and re-layouts: 1.54 us -> 0.64 us
    pallas_call x1, Pallas kernels: 42 us -> 39.8 us  [body(): pl.pallas_call(functools.partial(kernel, n_row, n_col, n_x), out_shape=ja...]
    unnamed x1, local copies, waits for them, and re-layouts: 1.54 us -> 0.64 us
where the time goes in v2:
time: 40.6 us; the launch traced here: 40.4 us
  Pallas kernels  39.8 us (98%)
  local copies, waits for them, and re-layouts  0.64 us (2%)
    pallas_call x1, Pallas kernels, body(): pl.pallas_call(functools.partial(kernel, n_row, n_col, n_x), out_shape=ja...  39.8 us

profile of v2, /device:TPU:0, one launch (start us, length us, event | category | flops | bytes accessed | tf_op | source)
XLA Modules:
  0.0 40.4 jit_solution(427992144776121894)
XLA Ops:
  0.0 39.8 %shard_map.46 = bf16[3,128,128]{2,1,0:T(8,128)(2,1)S(1)} custom-call(s32[1,128]{1,0:T(1,128)} %bitcast.6, s32[1,128]{1,0:T(1,128)} %bitcast.7, bf16[3,128,128]{2,1,0:T(8,128)(2,1)} %bitcast.5, bf16[1,1,128,128,128]{4,3,2,1,0:T(8,128)(2,1)} %tile_hbm.1), custom_call_target="tpu_custom_call" | custom-call | tf_op jit(solution)/shard_map/pallas_call | solution.py:286
  39.8 0.6 %copy.6 = bf16[384,128]{1,0:T(8,128)(2,1)} copy(bf16[384,128]{1,0:T(8,128)(2,1)S(1)} %bitcast.4) | data formatting | bytes 196608

commit v3 on v2

--- a/solution.py
+++ b/solution.py
@@ -9,7 +9,6 @@
 
 CHUNKS = 4
 BUILD = 8
-EARLY = 6
 ORDER = (
     "Z002", "Z000", "Z001", "S001", "Z010", "Z011", "Z012", "S011", "Z022", "X000", "X001",
     "Z021", "Z020", "S021", "X010", "Z032", "Z031", "X011", "Z030", "S031", "E000", "X020",
@@ -50,7 +49,7 @@
 
 
 def kernel(n_row, n_col, n_x, rows_hbm, cols_hbm, demand_hbm, tile_hbm, out, rows_ref, cols_ref, demand, tiles, weights, panel_a, panel_b, sums,
-           packed, landed, out_turned, plan_vector, plan, copy_sem, plan_sem, sx, rx, sz, rz, sr, rr):
+           packed, landed, out_turned, plan_vector, plan, met, copy_sem, plan_sem, sx, rx, sz, rz, sr, rr):
     n_z = n_col // n_x
     span, edge, columns = demand.shape
     slots = tiles.shape[0]
@@ -99,8 +98,9 @@
     def greet(r, c):
         pl.semaphore_signal(barrier, inc=1, device_id=(r, c), device_id_type=MESH)
 
-    for k in range(1, n_z):
-        greet(row, sent_to(k) * n_x + x)
+    above, below = z + 1 < n_z, z > 0
+    pl.when(above)(lambda: greet(row, col + n_x))
+    pl.when(below)(lambda: greet(row, col - n_x))
     for e in range(n_row - 1):
         greet(target(e), col)
     if n_x > 1:
@@ -117,21 +117,8 @@
         turned = jnp.transpose(demand[k])
         for c in range(chunks):
             panel_a[c, col * span + k] = turned[c * part:(c + 1) * part]
-    plan_copy.wait()
-    tile_copy.wait()
-
-    def merge(step, total):
-        for u in range(BUILD):
-            at = step * BUILD + u
-            keep = plan[2, at].astype(jnp.float32)
-            total = total * keep + tiles[plan[1, at]].astype(jnp.float32)
-            weights[at] = jnp.transpose(total.astype(weights.dtype))
-        return total
-
-    steps = slots // BUILD
-    early = steps * EARLY // 8
-    running = lax.fori_loop(0, early, merge, jnp.zeros((edge, edge), jnp.float32))
-    pl.semaphore_wait(barrier, n_z - 1 + n_row - 1 + (1 if n_x > 1 else 0))
+    greeted = n_row - 1 + (1 if n_x > 1 else 0) + above.astype(jnp.int32) + below.astype(jnp.int32)
+    pl.semaphore_wait(barrier, greeted)
 
     def block(p, c, zz, xx):
         return panels[p].at[c, pl.ds((zz * n_x + xx) * span, span)]
@@ -149,13 +136,13 @@
         here = block(p, c, got_from(k) if k else z, other)
         remote(here, here, sx.at[p, c, k], rx.at[p, c, k], (row, z * n_x + other)).wait_recv()
 
-    def along(p, c, k):
+    def along(p, c, zz):
         here = block(p, c, z, x)
-        return remote(here, here, sz.at[p, c, k - 1], rz.at[p, c, k - 1], (row, sent_to(k) * n_x + x))
-
-    def along_in(p, c, k):
-        here = block(p, c, got_from(k), x)
-        remote(here, here, sz.at[p, c, k - 1], rz.at[p, c, k - 1], (row, sent_to(k) * n_x + x)).wait_recv()
+        return remote(here, here, sz.at[p, c, zz], rz.at[p, c, z], (row, zz * n_x + x))
+
+    def along_in(p, c, zz):
+        here = block(p, c, zz, x)
+        remote(here, here, sz.at[p, c, zz], rz.at[p, c, zz], (row, zz * n_x + x)).wait_recv()
 
     def reduce_copy(p, c, e):
         return remote(packed.at[p, c, pl.ds(e * span, span)], landed.at[p, c, e], sr.at[p, c, e], rr.at[p, c, e],
@@ -165,11 +152,28 @@
         if n_x > 1:
             across(p, c, 0).start()
         for k in reversed(range(1, n_z)):
-            along(p, c, k).start()
+            along(p, c, sent_to(k)).start()
+
+    def spread(c, away):
+        pl.when(z + away < n_z)(lambda: along(0, c, z + away).start())
+        pl.when(z >= away)(lambda: along(0, c, z - away).start())
+
+    def vouch(away):
+        @pl.when(above & (z >= away - 1))
+        def _():
+            pl.semaphore_signal(met.at[0, away], inc=1, device_id=(row, col + n_x), device_id_type=MESH)
+
+        @pl.when(below & (z + away - 1 < n_z))
+        def _():
+            pl.semaphore_signal(met.at[1, away], inc=1, device_id=(row, col - n_x), device_id_type=MESH)
+
+    def vouched(away):
+        pl.when(z >= away)(lambda: pl.semaphore_wait(met.at[0, away], 1))
+        pl.when(z + away < n_z)(lambda: pl.semaphore_wait(met.at[1, away], 1))
 
     def relay(p, c, at):
         for k in range(1, n_z)[(n_z - 1) * at // 3:(n_z - 1) * (at + 1) // 3]:
-            along_in(p, c, k)
+            along_in(p, c, got_from(k))
             if n_x > 1:
                 across(p, c, k).start()
 
@@ -249,10 +253,36 @@
             launch(1, c)
 
     for c in range(chunks):
-        launch(0, c)
-
-    if early < steps:
-        lax.fori_loop(early, steps, merge, running)
+        if n_x > 1:
+            across(0, c, 0).start()
+        if n_z > 1 and c == 0:
+            spread(c, 1)
+    if n_z > 2:
+        vouch(2)
+    plan_copy.wait()
+    tile_copy.wait()
+
+    def merge(step, total):
+        for u in range(BUILD):
+            at = step * BUILD + u
+            keep = plan[2, at].astype(jnp.float32)
+            total = total * keep + tiles[plan[1, at]].astype(jnp.float32)
+            weights[at] = jnp.transpose(total.astype(weights.dtype))
+        return total
+
+    steps = slots // BUILD
+    share = steps // n_z
+    running = jnp.zeros((edge, edge), jnp.float32)
+    for away in range(2, n_z):
+        running = lax.fori_loop((away - 2) * share, (away - 1) * share, merge, running)
+        vouched(away)
+        spread(0, away)
+        if away + 1 < n_z:
+            vouch(away + 1)
+    for c in range(1, chunks):
+        for away in reversed(range(1, n_z)):
+            spread(c, away)
+    lax.fori_loop(max(n_z - 2, 0) * share, steps, merge, running)
 
     act = {"Z": relay, "S": near, "X": far, "E": collect}
     for op, p, c, at in order_of():
@@ -266,7 +296,7 @@
                 if n_x > 1:
                     across(p, c, k).wait_send()
                 if k:
-                    along(p, c, k).wait_send()
+                    along(p, c, sent_to(k)).wait_send()
             for e in range(n_row - 1):
                 reduce_copy(p, c, e).wait_send()
 
@@ -302,6 +332,7 @@
             pltpu.VMEM((span, columns, edge), kind),
             pltpu.VMEM((8, width), jnp.int32),
             pltpu.SMEM((8, width), jnp.int32),
+            pltpu.SemaphoreType.REGULAR((2, n_z + 1)),
             dma((4,)),
             dma,
             dma((2, CHUNKS, n_z)),

time: 40.6 us -> 39.3 us (0.968)
  Pallas kernels: 39.8 us -> 38.5 us
    pallas_call x1, Pallas kernels: 39.8 us -> 38.5 us  [body(): pl.pallas_call(functools.partial(kernel, n_row, n_col, n_x), out_shape=ja...]
where the time goes in v3:
time: 39.3 us; the launch traced here: 39.1 us
  Pallas kernels  38.5 us (98%)
  local copies, waits for them, and re-layouts  0.64 us (2%)
    pallas_call x1, Pallas kernels, body(): pl.pallas_call(functools.partial(kernel, n_row, n_col, n_x), out_shape=ja...  38.5 us

profile of v3, /device:TPU:0, one launch (start us, length us, event | category | flops | bytes accessed | tf_op | source)
XLA Modules:
  0.0 39.1 jit_solution(10837360486352725854)
XLA Ops:
  0.0 38.5 %shard_map.46 = bf16[3,128,128]{2,1,0:T(8,128)(2,1)S(1)} custom-call(s32[1,128]{1,0:T(1,128)} %bitcast.6, s32[1,128]{1,0:T(1,128)} %bitcast.7, bf16[3,128,128]{2,1,0:T(8,128)(2,1)} %bitcast.5, bf16[1,1,128,128,128]{4,3,2,1,0:T(8,128)(2,1)} %tile_hbm.1), custom_call_target="tpu_custom_call" | custom-call | tf_op jit(solution)/shard_map/pallas_call | solution.py:316
  38.5 0.6 %copy.6 = bf16[384,128]{1,0:T(8,128)(2,1)} copy(bf16[384,128]{1,0:T(8,128)(2,1)S(1)} %bitcast.4) | data formatting | bytes 196608
